TPU v7x, 32 devices: a whole 2x2x4 slice. The times are simulated.
32 devices in a mesh: gx: 4 (over x, core), gy: 8 (over z, y).
Axes of the slice: x: 2, y: 2, z: 4, core: 2. Of those that a mesh axis runs over, the one named last changes fastest.
Arguments:
- hot_ids: int32 [262144], P(('gx', 'gy')), may hold values from 0 to 2047
- hot_grads: bfloat16 [262144, 128], P(('gx', 'gy')), may hold values from -6 to 6
- cold_grads: bfloat16 [4, 8, 8, 512, 128], P('gx', 'gy'), may hold values from -6 to 6
- cold_slots: int32 [4, 8, 8, 512], P('gx', 'gy'), may hold values from 0 to 2047
- cold_counts: int32 [4, 8, 8], P('gx', 'gy'), may hold values from 1 to 512, as said below
Outputs:
- hot_grad: float32 [2048, 128], replicated
- cold_grad: float32 [4, 16384, 128], P('gx', 'gy')
Inputs may be any that keep to these rules, and one draw needn't show every extreme that they name: In each group g, some owner d receives cold_counts[g, s, d] = 512 from every s; loads per owner are skewed.
All inputs are finite; a program needn't handle non-finite values.
Results may differ from a plain program's by a relative error of at most 0.0003.
Values may be sent and summed in bfloat16 or wider, within the bound.
A program may use at most 64 MiB of HBM per device.

v0:
```python
import math
import jax
import jax.numpy as jnp
from jax import lax
from jax.sharding import PartitionSpec as P

HOT = 2048
OWN_ROWS = 2048


def onehot_sum(row_ids, row_data, table_size, block_rows):
    turns = row_ids.shape[0] // block_rows
    id_blocks = row_ids.reshape(turns, block_rows)
    data_blocks = row_data.reshape(turns, block_rows, row_data.shape[1])
    table_iota = lax.broadcasted_iota(jnp.int32, (table_size, block_rows), 0)

    def add_block(total, pieces):
        ids_here, data_here = pieces
        selector = (table_iota == ids_here[None, :]).astype(jnp.bfloat16)
        return (total + jnp.dot(selector, data_here, preferred_element_type=jnp.float32), None)

    start = jnp.zeros((table_size, row_data.shape[1]), jnp.float32)
    total, unused = lax.scan(add_block, start, (id_blocks, data_blocks))
    return total


def hot_part(hot_ids, hot_grads):
    hot_rows = HOT
    block_rows = math.gcd(hot_ids.shape[0], 2048)
    local_sum = onehot_sum(hot_ids, hot_grads, hot_rows, block_rows)
    factor = (hot_rows / (hot_ids.shape[0] * lax.axis_size("gx") * lax.axis_size("gy"))) ** 0.5
    shared = lax.psum_scatter(local_sum, "gy", scatter_dimension=0, tiled=True)
    shared = lax.psum(shared, "gx")
    total = lax.all_gather(shared, "gy", axis=0, tiled=True)
    return total * factor


def cold_part(cold_grads, cold_slots, cold_counts):
    owners, capacity, width = (cold_grads.shape[2], cold_grads.shape[3], cold_grads.shape[4])
    grads_here = cold_grads.reshape(owners, capacity, width)
    slots_here = cold_slots.reshape(owners, capacity)
    counts_here = cold_counts.reshape(owners)
    places = lax.broadcasted_iota(jnp.int32, (owners, capacity), 1)
    valid = places < counts_here[:, None]
    payload = jnp.where(valid[:, :, None], grads_here, jnp.zeros_like(grads_here))
    got_rows, got_slots = (
        lax.all_to_all(payload, "gy", split_axis=0, concat_axis=0, tiled=True),
        lax.all_to_all(slots_here, "gy", split_axis=0, concat_axis=0, tiled=True),
    )
    total_rows = owners * capacity
    block_rows = math.gcd(total_rows, 1024)
    table = onehot_sum(
        got_slots.reshape(total_rows), got_rows.reshape(total_rows, width), OWN_ROWS, block_rows
    )
    return table.reshape(1, OWN_ROWS, width)


def per_device(hot_ids, hot_grads, cold_grads, cold_slots, cold_counts):
    hot_grad = hot_part(hot_ids, hot_grads)
    cold_grad = cold_part(cold_grads, cold_slots, cold_counts)
    return (hot_grad, cold_grad)


def solution(mesh):
    return jax.shard_map(
        per_device,
        mesh=mesh,
        in_specs=(
            P(("gx", "gy")),
            P(("gx", "gy"), None),
            P("gx", "gy", None, None, None),
            P("gx", "gy", None, None),
            P("gx", "gy", None),
        ),
        out_specs=(P(), P("gx", "gy", None)),
        check_vma=False,
    )
```

profile of v0, /device:TPU:0, one launch (start us, length us, event | category | flops | bytes accessed | tf_op | source)
XLA Modules:
  0.0 185.8 jit_solution(4274179711939193013)
XLA Ops:
  7.2 0.0 reduce-scatter.2.cloned.1.call-start
  7.2 0.8 reshape.43
  8.0 0.0 copy-start.2
  8.0 0.0 copy-start.3
  8.0 0.0 copy-start
  8.0 17.7 %while.22 = (s32[]{:T(128)}, f32[2048,128]{1,0:T(8,128)S(1)}, s32[4,2048]{1,0:T(4,128)S(1)}, bf16[4,2048,128]{2,1,0:T(8,128)(2,1)}, s32[]{:T(128)}, /*index=5*/s32[]{:T(128)}) while((s32[]{:T(128)}, f32[2048,128]{1,0:T(8,128)S(1)}, s32[4,2048]{1,0:T(4,128)S(1)}, bf16[4,2048,128]{2,1,0:T(8,128)(2,1)}, s32[]{:T(128)}, ...), condition=%wide.region_1.2_spmd.clone, body=%wide.region_0.1_spmd.clone.sunk | while | flops 1078460416 | bytes 2646611 | solution.py:23
  8.1 4.4 %fusion.21 = f32[2048,128]{1,0:T(8,128)S(1)} fusion(s32[2048]{0:T(1024)S(1)} %bitcast.25, f32[2048,128]{1,0:T(8,128)S(1)} %get-tuple-element.165, bf16[4,2048,128]{2,1,0:T(8,128)(2,1)} %get-tuple-element.173, s32[]{:T(128)} %get-tuple-element.164, pred[]{:T(512)S(6)} %compare.6), kind=kOutput, calls=%fused_computation.5.clone.1 | convolution fusion | flops 1078460416 | bytes 2630145 | tf_op jit(solution)/shard_map/while/body/eval_jaxpr/dot_general | solution.py:20
  12.6 4.4 %fusion.21 = f32[2048,128]{1,0:T(8,128)S(1)} fusion(s32[2048]{0:T(1024)S(1)} %bitcast.25, f32[2048,128]{1,0:T(8,128)S(1)} %get-tuple-element.165, bf16[4,2048,128]{2,1,0:T(8,128)(2,1)} %get-tuple-element.173, s32[]{:T(128)} %get-tuple-element.164, pred[]{:T(512)S(6)} %compare.6), kind=kOutput, calls=%fused_computation.5.clone.1 | convolution fusion | flops 1078460416 | bytes 2630145 | tf_op jit(solution)/shard_map/while/body/eval_jaxpr/dot_general | solution.py:20
  17.0 4.4 %fusion.21 = f32[2048,128]{1,0:T(8,128)S(1)} fusion(s32[2048]{0:T(1024)S(1)} %bitcast.25, f32[2048,128]{1,0:T(8,128)S(1)} %get-tuple-element.165, bf16[4,2048,128]{2,1,0:T(8,128)(2,1)} %get-tuple-element.173, s32[]{:T(128)} %get-tuple-element.164, pred[]{:T(512)S(6)} %compare.6), kind=kOutput, calls=%fused_computation.5.clone.1 | convolution fusion | flops 1078460416 | bytes 2630145 | tf_op jit(solution)/shard_map/while/body/eval_jaxpr/dot_general | solution.py:20
  21.4 4.4 %fusion.21 = f32[2048,128]{1,0:T(8,128)S(1)} fusion(s32[2048]{0:T(1024)S(1)} %bitcast.25, f32[2048,128]{1,0:T(8,128)S(1)} %get-tuple-element.165, bf16[4,2048,128]{2,1,0:T(8,128)(2,1)} %get-tuple-element.173, s32[]{:T(128)} %get-tuple-element.164, pred[]{:T(512)S(6)} %compare.6), kind=kOutput, calls=%fused_computation.5.clone.1 | convolution fusion | flops 1078460416 | bytes 2630145 | tf_op jit(solution)/shard_map/while/body/eval_jaxpr/dot_general | solution.py:20
  25.7 0.0 copy-start.1
  25.8 1.0 copy-done.1
  26.7 0.0 reduce-scatter.2.cloned.1.call-update
  26.7 0.0 copy-done.2
  26.8 0.6 all_to_all.9
  27.4 7.3 %all-to-all-start = ((s32[8,1,512]{2,1,0:T(1,128)}), s32[8,1,512]{2,1,0:T(1,128)S(1)}, u32[]{:S(2)}, u32[]{:S(2)}) async-start(s32[8,1,512]{2,1,0:T(1,128)} %all_to_all.9), calls=%async_computation.1 | async-start | bytes 32768 | tf_op jit(solution)/shard_map/all_to_all | solution.py:48
  34.7 0.0 copy-done.3
  34.7 0.1 iota_compare_fusion.8
  34.8 0.0 copy-done
  34.8 1.5 bitcast_select_fusion
  36.2 5.1 %all-to-all-done = s32[8,1,512]{2,1,0:T(1,128)S(1)} async-done(((s32[8,1,512]{2,1,0:T(1,128)}), s32[8,1,512]{2,1,0:T(1,128)S(1)}, u32[]{:S(2)}, u32[]{:S(2)}) %all-to-all-start) | async-done | bytes 16416 | tf_op jit(solution)/shard_map/all_to_all | solution.py:48
  41.3 3.6 %all-to-all-start.1 = ((bf16[8,512,128]{2,1,0:T(8,128)(2,1)}), bf16[8,512,128]{2,1,0:T(8,128)(2,1)S(1)}, u32[]{:S(2)}, u32[]{:S(2)}) async-start(bf16[8,512,128]{2,1,0:T(8,128)(2,1)} %bitcast_select_fusion), calls=%async_computation.2 | async-start | bytes 2097152 | tf_op jit(solution)/shard_map/all_to_all | solution.py:47
  44.9 0.0 all-reduce.2.cloned.1.call-start
  44.9 56.6 %reduce-scatter.2.cloned.1.call-done = f32[256,128]{1,0:T(8,128)} async-done(((f32[2048,128]{1,0:T(8,128)}), f32[256,128]{1,0:T(8,128)}) %reduce-scatter.2.cloned.1.call-update) | async-done | bytes 131088 | tf_op jit(solution)/shard_map/reduce_scatter | solution.py:32
  101.6 0.0 all-reduce.2.cloned.1.call-update
  101.6 0.0 all-gather.2.cloned.1.call-start
  101.6 32.9 %all-reduce.2.cloned.1.call-done = f32[256,128]{1,0:T(8,128)} async-done(((f32[256,128]{1,0:T(8,128)}), f32[256,128]{1,0:T(8,128)}) %all-reduce.2.cloned.1.call-update) | async-done | bytes 131088 | tf_op jit(solution)/shard_map/psum | solution.py:33
  134.6 0.0 all-gather.2.cloned.1.call-update
  134.7 0.0 all-to-all-done.1
  134.7 7.3 %while.23 = (s32[]{:T(128)}, f32[2048,128]{1,0:T(8,128)S(1)}, s32[4,1024]{1,0:T(4,128)S(1)}, bf16[4,1024,128]{2,1,0:T(8,128)(2,1)S(1)}, s32[]{:T(128)}, /*index=5*/s32[]{:T(128)}) while((s32[]{:T(128)}, f32[2048,128]{1,0:T(8,128)S(1)}, s32[4,1024]{1,0:T(4,128)S(1)}, bf16[4,1024,128]{2,1,0:T(8,128)(2,1)S(1)}, s32[]{:T(128)}, ...), condition=%wide.region_5.6_spmd.clone, body=%wide.region_4.5_spmd.clone.sunk | while | flops 539492352 | bytes 2371671 | solution.py:23
  134.7 1.8 fusion.23
  136.5 1.8 fusion.23
  138.4 1.8 fusion.23
  140.2 1.8 fusion.23
  142.0 0.0 copy-start.4
  142.0 35.0 %all-gather.2.cloned.1.call-done = f32[2048,128]{1,0:T(8,128)} async-done(((f32[256,128]{1,0:T(8,128)}), f32[2048,128]{1,0:T(8,128)}) %all-gather.2.cloned.1.call-update) | async-done | bytes 1048592 | tf_op jit(solution)/shard_map/all_gather | solution.py:34
  177.0 2.3 %broadcast_multiply_fusion = f32[2048,128]{1,0:T(8,128)} fusion(f32[2048,128]{1,0:T(8,128)} %all-gather.2.cloned.1.call-done), kind=kLoop, calls=%fused_computation.19 | loop fusion | flops 262144 | bytes 2097152 | tf_op jit(solution)/shard_map/mul | solution.py:35
  179.3 0.0 copy-done.4
  (12 shorter events, 0.1 us)
Async XLA Ops:
  7.2 94.4 %reduce-scatter.2.cloned.1.call-start = ((), (), s32[]{:S(2)}) async-start(), calls=%async_computation.3 | async-start | bytes 1179648 | tf_op jit(solution)/shard_map/reduce_scatter | solution.py:32
  8.0 18.8 %copy-start.2 = (s32[1,1,8,512]{3,2,1,0:T(8,128)S(1)}, s32[1,1,8,512]{3,2,1,0:T(8,128)}, u32[]{:S(2)}) copy-start(s32[1,1,8,512]{3,2,1,0:T(8,128)} %param.12) | copy-start | bytes 49156
  8.0 26.7 %copy-start.3 = (s32[1,1,8]{2,1,0:T(1,128)S(1)}, s32[1,1,8]{2,1,0:T(1,128)}, u32[]{:S(2)}) copy-start(s32[1,1,8]{2,1,0:T(1,128)} %param.13) | copy-start | bytes 100
  8.0 26.7 %copy-start = (bf16[1,1,8,512,128]{4,3,2,1,0:T(8,128)(2,1)S(1)}, bf16[1,1,8,512,128]{4,3,2,1,0:T(8,128)(2,1)}, u32[]{:S(2)}) copy-start(bf16[1,1,8,512,128]{4,3,2,1,0:T(8,128)(2,1)} %param.11) | copy-start | bytes 3145732
  25.7 1.0 copy-start.1
  27.4 13.9 %all-to-all-start = ((s32[8,1,512]{2,1,0:T(1,128)}), s32[8,1,512]{2,1,0:T(1,128)S(1)}, u32[]{:S(2)}, u32[]{:S(2)}) async-start(s32[8,1,512]{2,1,0:T(1,128)} %all_to_all.9), calls=%async_computation.1 | async-start | bytes 32768 | tf_op jit(solution)/shard_map/all_to_all | solution.py:48
  41.3 93.4 %all-to-all-start.1 = ((bf16[8,512,128]{2,1,0:T(8,128)(2,1)}), bf16[8,512,128]{2,1,0:T(8,128)(2,1)S(1)}, u32[]{:S(2)}, u32[]{:S(2)}) async-start(bf16[8,512,128]{2,1,0:T(8,128)(2,1)} %bitcast_select_fusion), calls=%async_computation.2 | async-start | bytes 2097152 | tf_op jit(solution)/shard_map/all_to_all | solution.py:47
  44.9 89.7 %all-reduce.2.cloned.1.call-start = ((), (), s32[]{:S(2)}) async-start(), calls=%async_computation.4 | async-start | bytes 262144 | tf_op jit(solution)/shard_map/psum | solution.py:33
  101.6 75.4 %all-gather.2.cloned.1.call-start = ((), (), s32[]{:S(2)}) async-start(), calls=%async_computation.5 | async-start | bytes 1179648 | tf_op jit(solution)/shard_map/all_gather | solution.py:34
  142.0 37.3 %copy-start.4 = (f32[2048,128]{1,0:T(8,128)}, f32[2048,128]{1,0:T(8,128)S(1)}, u32[]{:S(2)}) copy-start(f32[2048,128]{1,0:T(8,128)S(1)} %get-tuple-element.57) | copy-start | bytes 3145732
Sparse Core Ops, SparseCore 0:
  26.9 74.6 reduce-scatter.1
  103.9 30.6 all-reduce.1
  136.7 40.2 all-gather.1
where the time goes:
time: 186 us
  waiting for transfers between devices  130 us (70%)
  matrix products  24.7 us (13%)
  between operations  13.9 us (7%)
  starting transfers between devices  11 us (6%)
  other arithmetic  3.89 us (2%)
  local copies, waits for them, and re-layouts  2.47 us (1%)
    reduce_scatter x1, waiting for transfers between devices, hot_part(): shared = lax.psum_scatter(local_sum, 'gy', scatter_dimension=0, tiled=True)  56.6 us
    all_gather x1, waiting for transfers between devices, hot_part(): total = lax.all_gather(shared, 'gy', axis=0, tiled=True)  35 us
    psum x1, waiting for transfers between devices, hot_part(): shared = lax.psum(shared, 'gx')  32.9 us
    dot_general x8, matrix products, add_block(): jnp.dot(selector, data_here, preferred_element_type=jnp.float32)  24.7 us
    all_to_all x1, starting transfers between devices, cold_part(): lax.all_to_all(slots_here, 'gy', split_axis=0, concat_axis=0, tiled=True)  7.31 us
    all_to_all x1, waiting for transfers between devices, cold_part(): lax.all_to_all(slots_here, 'gy', split_axis=0, concat_axis=0, tiled=True)  5.07 us
  transfers between devices with their start and end apart: 5, of which 4 were waited for; matrix products, arithmetic and copies ran while one was open for 5% of the time, Pallas kernels for 0%

commit v1 on v0

--- a/solution.py
+++ b/solution.py
@@ -31,7 +31,12 @@
     factor = (hot_rows / (hot_ids.shape[0] * lax.axis_size("gx") * lax.axis_size("gy"))) ** 0.5
     shared = lax.psum_scatter(local_sum, "gy", scatter_dimension=0, tiled=True)
     shared = lax.psum(shared, "gx")
-    total = lax.all_gather(shared, "gy", axis=0, tiled=True)
+    ring = [shared]
+    for hop in range(7):
+        ring.append(lax.ppermute(ring[-1], "gy", [(dev, (dev + 1) % 8) for dev in range(8)]))
+    total = jnp.roll(
+        jnp.concatenate(ring[::-1], axis=0), (lax.axis_index("gy") + 1) * ring[0].shape[0], axis=0
+    )
     return total * factor
 
 

time: 186 us -> 199 us (1.070)
  waiting for transfers between devices: 130 us -> 141 us
    ppermute x0 -> x7, waiting for transfers between devices: none -> 46.7 us  [hot_part(): lax.ppermute(ring[-1], 'gy', [(dev, (dev + 1) % 8) for dev in range(8)])]
    all_gather x1 -> x0, waiting for transfers between devices: 35 us -> none  [hot_part(): total = lax.all_gather(shared, 'gy', axis=0, tiled=True)]
  transfers between devices with their start and end apart: 5 -> 11, of which waited for: 4 -> 10; matrix products, arithmetic and copies ran while one was open for 5% -> 4% of each run, Pallas kernels for 0% -> 0%
where the time goes in v1:
time: 199 us
  waiting for transfers between devices  141 us (71%)
  matrix products  24.7 us (12%)
  between operations  14.3 us (7%)
  starting transfers between devices  12.4 us (6%)
  local copies, waits for them, and re-layouts  2.97 us (1%)
  other arithmetic  2.66 us (1%)
    reduce_scatter x1, waiting for transfers between devices, hot_part(): shared = lax.psum_scatter(local_sum, 'gy', scatter_dimension=0, tiled=True)  56.6 us
    ppermute x7, waiting for transfers between devices, hot_part(): lax.ppermute(ring[-1], 'gy', [(dev, (dev + 1) % 8) for dev in range(8)])  46.7 us
    psum x1, waiting for transfers between devices, hot_part(): shared = lax.psum(shared, 'gx')  33 us
    dot_general x8, matrix products, add_block(): jnp.dot(selector, data_here, preferred_element_type=jnp.float32)  24.7 us
    all_to_all x1, starting transfers between devices, cold_part(): lax.all_to_all(slots_here, 'gy', split_axis=0, concat_axis=0, tiled=True)  7.31 us
    all_to_all x1, waiting for transfers between devices, cold_part(): lax.all_to_all(slots_here, 'gy', split_axis=0, concat_axis=0, tiled=True)  5.07 us
  transfers between devices with their start and end apart: 11, of which 10 were waited for; matrix products, arithmetic and copies ran while one was open for 4% of the time, Pallas kernels for 0%

profile of v1, /device:TPU:0, one launch (start us, length us, event | category | flops | bytes accessed | tf_op | source)
XLA Modules:
  0.0 198.7 jit_solution(11154275508790630177)
XLA Ops:
  7.2 0.0 reduce-scatter.2.cloned.1.call-start
  7.2 0.8 reshape.43
  8.0 0.0 copy-start.3
  8.0 0.0 copy-start.4
  8.0 0.0 copy-start
  8.0 17.7 %while.22 = (s32[]{:T(128)}, f32[2048,128]{1,0:T(8,128)S(1)}, s32[4,2048]{1,0:T(4,128)S(1)}, bf16[4,2048,128]{2,1,0:T(8,128)(2,1)}, s32[]{:T(128)}, /*index=5*/s32[]{:T(128)}) while((s32[]{:T(128)}, f32[2048,128]{1,0:T(8,128)S(1)}, s32[4,2048]{1,0:T(4,128)S(1)}, bf16[4,2048,128]{2,1,0:T(8,128)(2,1)}, s32[]{:T(128)}, ...), condition=%wide.region_1.2_spmd.clone, body=%wide.region_0.1_spmd.clone.sunk | while | flops 1078460416 | bytes 2646611 | solution.py:23
  8.1 4.4 %fusion.21 = f32[2048,128]{1,0:T(8,128)S(1)} fusion(s32[2048]{0:T(1024)S(1)} %bitcast.25, f32[2048,128]{1,0:T(8,128)S(1)} %get-tuple-element.165, bf16[4,2048,128]{2,1,0:T(8,128)(2,1)} %get-tuple-element.173, s32[]{:T(128)} %get-tuple-element.164, pred[]{:T(512)S(6)} %compare.7), kind=kOutput, calls=%fused_computation.5.clone.1 | convolution fusion | flops 1078460416 | bytes 2630145 | tf_op jit(solution)/shard_map/while/body/eval_jaxpr/dot_general | solution.py:20
  12.6 4.4 %fusion.21 = f32[2048,128]{1,0:T(8,128)S(1)} fusion(s32[2048]{0:T(1024)S(1)} %bitcast.25, f32[2048,128]{1,0:T(8,128)S(1)} %get-tuple-element.165, bf16[4,2048,128]{2,1,0:T(8,128)(2,1)} %get-tuple-element.173, s32[]{:T(128)} %get-tuple-element.164, pred[]{:T(512)S(6)} %compare.7), kind=kOutput, calls=%fused_computation.5.clone.1 | convolution fusion | flops 1078460416 | bytes 2630145 | tf_op jit(solution)/shard_map/while/body/eval_jaxpr/dot_general | solution.py:20
  17.0 4.4 %fusion.21 = f32[2048,128]{1,0:T(8,128)S(1)} fusion(s32[2048]{0:T(1024)S(1)} %bitcast.25, f32[2048,128]{1,0:T(8,128)S(1)} %get-tuple-element.165, bf16[4,2048,128]{2,1,0:T(8,128)(2,1)} %get-tuple-element.173, s32[]{:T(128)} %get-tuple-element.164, pred[]{:T(512)S(6)} %compare.7), kind=kOutput, calls=%fused_computation.5.clone.1 | convolution fusion | flops 1078460416 | bytes 2630145 | tf_op jit(solution)/shard_map/while/body/eval_jaxpr/dot_general | solution.py:20
  21.4 4.4 %fusion.21 = f32[2048,128]{1,0:T(8,128)S(1)} fusion(s32[2048]{0:T(1024)S(1)} %bitcast.25, f32[2048,128]{1,0:T(8,128)S(1)} %get-tuple-element.165, bf16[4,2048,128]{2,1,0:T(8,128)(2,1)} %get-tuple-element.173, s32[]{:T(128)} %get-tuple-element.164, pred[]{:T(512)S(6)} %compare.7), kind=kOutput, calls=%fused_computation.5.clone.1 | convolution fusion | flops 1078460416 | bytes 2630145 | tf_op jit(solution)/shard_map/while/body/eval_jaxpr/dot_general | solution.py:20
  25.7 0.0 copy-start.1
  25.8 1.0 copy-done.1
  26.7 0.0 reduce-scatter.2.cloned.1.call-update
  26.7 0.0 copy-done.3
  26.8 0.6 all_to_all.9
  27.4 7.3 %all-to-all-start = ((s32[8,1,512]{2,1,0:T(1,128)}), s32[8,1,512]{2,1,0:T(1,128)S(1)}, u32[]{:S(2)}, u32[]{:S(2)}) async-start(s32[8,1,512]{2,1,0:T(1,128)} %all_to_all.9), calls=%async_computation.1 | async-start | bytes 32768 | tf_op jit(solution)/shard_map/all_to_all | solution.py:53
  34.7 0.0 copy-done.4
  34.7 0.1 iota_compare_fusion.8
  34.8 1.5 bitcast_select_fusion
  36.2 5.1 %all-to-all-done = s32[8,1,512]{2,1,0:T(1,128)S(1)} async-done(((s32[8,1,512]{2,1,0:T(1,128)}), s32[8,1,512]{2,1,0:T(1,128)S(1)}, u32[]{:S(2)}, u32[]{:S(2)}) %all-to-all-start) | async-done | bytes 16416 | tf_op jit(solution)/shard_map/all_to_all | solution.py:53
  41.3 3.6 %all-to-all-start.1 = ((bf16[8,512,128]{2,1,0:T(8,128)(2,1)}), bf16[8,512,128]{2,1,0:T(8,128)(2,1)S(1)}, u32[]{:S(2)}, u32[]{:S(2)}) async-start(bf16[8,512,128]{2,1,0:T(8,128)(2,1)} %bitcast_select_fusion), calls=%async_computation.2 | async-start | bytes 2097152 | tf_op jit(solution)/shard_map/all_to_all | solution.py:52
  44.9 0.0 all-reduce.2.cloned.1.call-start
  44.9 56.6 %reduce-scatter.2.cloned.1.call-done = f32[256,128]{1,0:T(8,128)} async-done(((f32[2048,128]{1,0:T(8,128)}), f32[256,128]{1,0:T(8,128)}) %reduce-scatter.2.cloned.1.call-update) | async-done | bytes 131088 | tf_op jit(solution)/shard_map/reduce_scatter | solution.py:32
  101.5 0.0 all-reduce.2.cloned.1.call-update
  101.6 33.0 %all-reduce.2.cloned.1.call-done = f32[256,128]{1,0:T(8,128)} async-done(((f32[256,128]{1,0:T(8,128)}), f32[256,128]{1,0:T(8,128)}) %all-reduce.2.cloned.1.call-update) | async-done | bytes 131088 | tf_op jit(solution)/shard_map/psum | solution.py:33
  134.6 1.5 collective-permute-start
  136.0 6.4 %collective-permute-done = f32[256,128]{1,0:T(8,128)S(1)} collective-permute-done((f32[256,128]{1,0:T(8,128)}, f32[256,128]{1,0:T(8,128)S(1)}, u32[]{:S(2)}, u32[]{:S(2)}) %collective-permute-start) | collective-permute-done | bytes 131104 | tf_op jit(solution)/shard_map/ppermute | solution.py:36
  142.4 0.0 collective-permute-start.1
  142.4 7.7 %collective-permute-done.1 = f32[256,128]{1,0:T(8,128)S(1)} collective-permute-done((f32[256,128]{1,0:T(8,128)S(1)}, f32[256,128]{1,0:T(8,128)S(1)}, u32[]{:S(2)}, u32[]{:S(2)}) %collective-permute-start.1) | collective-permute-done | bytes 131104 | tf_op jit(solution)/shard_map/ppermute | solution.py:36
  150.1 0.0 collective-permute-start.2
  150.1 7.7 %collective-permute-done.2 = f32[256,128]{1,0:T(8,128)S(1)} collective-permute-done((f32[256,128]{1,0:T(8,128)S(1)}, f32[256,128]{1,0:T(8,128)S(1)}, u32[]{:S(2)}, u32[]{:S(2)}) %collective-permute-start.2) | collective-permute-done | bytes 131104 | tf_op jit(solution)/shard_map/ppermute | solution.py:36
  157.8 0.0 collective-permute-start.3
  157.8 8.4 %collective-permute-done.3 = f32[256,128]{1,0:T(8,128)S(1)} collective-permute-done((f32[256,128]{1,0:T(8,128)S(1)}, f32[256,128]{1,0:T(8,128)S(1)}, u32[]{:S(2)}, u32[]{:S(2)}) %collective-permute-start.3) | collective-permute-done | bytes 131104 | tf_op jit(solution)/shard_map/ppermute | solution.py:36
  166.2 0.0 collective-permute-start.4
  166.2 8.6 %collective-permute-done.4 = f32[256,128]{1,0:T(8,128)S(1)} collective-permute-done((f32[256,128]{1,0:T(8,128)S(1)}, f32[256,128]{1,0:T(8,128)S(1)}, u32[]{:S(2)}, u32[]{:S(2)}) %collective-permute-start.4) | collective-permute-done | bytes 131104 | tf_op jit(solution)/shard_map/ppermute | solution.py:36
  174.8 0.0 collective-permute-start.5
  174.8 7.7 %collective-permute-done.5 = f32[256,128]{1,0:T(8,128)S(1)} collective-permute-done((f32[256,128]{1,0:T(8,128)S(1)}, f32[256,128]{1,0:T(8,128)S(1)}, u32[]{:S(2)}, u32[]{:S(2)}) %collective-permute-start.5) | collective-permute-done | bytes 131104 | tf_op jit(solution)/shard_map/ppermute | solution.py:36
  182.5 0.0 collective-permute-start.6
  182.5 0.0 all-to-all-done.1
  182.5 7.3 %while.23 = (s32[]{:T(128)}, f32[2048,128]{1,0:T(8,128)S(1)}, s32[4,1024]{1,0:T(4,128)S(1)}, bf16[4,1024,128]{2,1,0:T(8,128)(2,1)S(1)}, s32[]{:T(128)}, /*index=5*/s32[]{:T(128)}) while((s32[]{:T(128)}, f32[2048,128]{1,0:T(8,128)S(1)}, s32[4,1024]{1,0:T(4,128)S(1)}, bf16[4,1024,128]{2,1,0:T(8,128)(2,1)S(1)}, s32[]{:T(128)}, ...), condition=%wide.region_5.6_spmd.clone, body=%wide.region_4.5_spmd.clone.sunk | while | flops 539492352 | bytes 2371671 | solution.py:23
  182.5 1.8 fusion.23
  184.4 1.8 fusion.23
  186.2 1.8 fusion.23
  188.0 1.8 fusion.23
  189.8 0.0 copy-start.5
  189.8 0.3 collective-permute-done.6
  190.5 0.3 copy-done.5
  190.8 1.1 dynamic-slice_multiply_fusion
  (31 shorter events, 0.3 us)
Async XLA Ops:
  7.2 94.4 %reduce-scatter.2.cloned.1.call-start = ((), (), s32[]{:S(2)}) async-start(), calls=%async_computation.3 | async-start | bytes 1179648 | tf_op jit(solution)/shard_map/reduce_scatter | solution.py:32
  8.0 18.7 %copy-start.3 = (s32[1,1,8,512]{3,2,1,0:T(8,128)S(1)}, s32[1,1,8,512]{3,2,1,0:T(8,128)}, u32[]{:S(2)}) copy-start(s32[1,1,8,512]{3,2,1,0:T(8,128)} %param.12) | copy-start | bytes 49156
  8.0 26.7 %copy-start.4 = (s32[1,1,8]{2,1,0:T(1,128)S(1)}, s32[1,1,8]{2,1,0:T(1,128)}, u32[]{:S(2)}) copy-start(s32[1,1,8]{2,1,0:T(1,128)} %param.13) | copy-start | bytes 100
  8.0 26.7 %copy-start = (bf16[1,1,8,512,128]{4,3,2,1,0:T(8,128)(2,1)S(1)}, bf16[1,1,8,512,128]{4,3,2,1,0:T(8,128)(2,1)}, u32[]{:S(2)}) copy-start(bf16[1,1,8,512,128]{4,3,2,1,0:T(8,128)(2,1)} %param.11) | copy-start | bytes 3145732
  25.7 1.0 copy-start.1
  27.4 13.9 %all-to-all-start = ((s32[8,1,512]{2,1,0:T(1,128)}), s32[8,1,512]{2,1,0:T(1,128)S(1)}, u32[]{:S(2)}, u32[]{:S(2)}) async-start(s32[8,1,512]{2,1,0:T(1,128)} %all_to_all.9), calls=%async_computation.1 | async-start | bytes 32768 | tf_op jit(solution)/shard_map/all_to_all | solution.py:53
  41.3 141.2 %all-to-all-start.1 = ((bf16[8,512,128]{2,1,0:T(8,128)(2,1)}), bf16[8,512,128]{2,1,0:T(8,128)(2,1)S(1)}, u32[]{:S(2)}, u32[]{:S(2)}) async-start(bf16[8,512,128]{2,1,0:T(8,128)(2,1)} %bitcast_select_fusion), calls=%async_computation.2 | async-start | bytes 2097152 | tf_op jit(solution)/shard_map/all_to_all | solution.py:52
  44.9 89.7 %all-reduce.2.cloned.1.call-start = ((), (), s32[]{:S(2)}) async-start(), calls=%async_computation.4 | async-start | bytes 262144 | tf_op jit(solution)/shard_map/psum | solution.py:33
  134.6 7.9 %collective-permute-start = (f32[256,128]{1,0:T(8,128)}, f32[256,128]{1,0:T(8,128)S(1)}, u32[]{:S(2)}, u32[]{:S(2)}) collective-permute-start(f32[256,128]{1,0:T(8,128)} %all-reduce.2.cloned.1.call-done), channel_id=1, source_target_pairs={{0,1},{1,2},{2,3},{3,4},{4,5},{5,6},{6,7},{7,0},{8,9},{9,10},{10,1... | collective-permute-start | bytes 393224 | tf_op jit(solution)/shard_map/ppermute | solution.py:36
  142.4 7.7 %collective-permute-start.1 = (f32[256,128]{1,0:T(8,128)S(1)}, f32[256,128]{1,0:T(8,128)S(1)}, u32[]{:S(2)}, u32[]{:S(2)}) collective-permute-start(f32[256,128]{1,0:T(8,128)S(1)} %collective-permute-done), channel_id=1, source_target_pairs={{0,1},{1,2},{2,3},{3,4},{4,5},{5,6},{6,7},{7,0},{8,9},{9,10},{10,1... | collective-permute-start | bytes 393224 | tf_op jit(solution)/shard_map/ppermute | solution.py:36
  150.1 7.7 %collective-permute-start.2 = (f32[256,128]{1,0:T(8,128)S(1)}, f32[256,128]{1,0:T(8,128)S(1)}, u32[]{:S(2)}, u32[]{:S(2)}) collective-permute-start(f32[256,128]{1,0:T(8,128)S(1)} %collective-permute-done.1), channel_id=1, source_target_pairs={{0,1},{1,2},{2,3},{3,4},{4,5},{5,6},{6,7},{7,0},{8,9},{9,10},{10,1... | collective-permute-start | bytes 393224 | tf_op jit(solution)/shard_map/ppermute | solution.py:36
  157.8 8.4 %collective-permute-start.3 = (f32[256,128]{1,0:T(8,128)S(1)}, f32[256,128]{1,0:T(8,128)S(1)}, u32[]{:S(2)}, u32[]{:S(2)}) collective-permute-start(f32[256,128]{1,0:T(8,128)S(1)} %collective-permute-done.2), channel_id=1, source_target_pairs={{0,1},{1,2},{2,3},{3,4},{4,5},{5,6},{6,7},{7,0},{8,9},{9,10},{10,1... | collective-permute-start | bytes 393224 | tf_op jit(solution)/shard_map/ppermute | solution.py:36
  166.2 8.6 %collective-permute-start.4 = (f32[256,128]{1,0:T(8,128)S(1)}, f32[256,128]{1,0:T(8,128)S(1)}, u32[]{:S(2)}, u32[]{:S(2)}) collective-permute-start(f32[256,128]{1,0:T(8,128)S(1)} %collective-permute-done.3), channel_id=1, source_target_pairs={{0,1},{1,2},{2,3},{3,4},{4,5},{5,6},{6,7},{7,0},{8,9},{9,10},{10,1... | collective-permute-start | bytes 393224 | tf_op jit(solution)/shard_map/ppermute | solution.py:36
  174.8 7.7 %collective-permute-start.5 = (f32[256,128]{1,0:T(8,128)S(1)}, f32[256,128]{1,0:T(8,128)S(1)}, u32[]{:S(2)}, u32[]{:S(2)}) collective-permute-start(f32[256,128]{1,0:T(8,128)S(1)} %collective-permute-done.4), channel_id=1, source_target_pairs={{0,1},{1,2},{2,3},{3,4},{4,5},{5,6},{6,7},{7,0},{8,9},{9,10},{10,1... | collective-permute-start | bytes 393224 | tf_op jit(solution)/shard_map/ppermute | solution.py:36
  182.5 7.7 %collective-permute-start.6 = (f32[256,128]{1,0:T(8,128)S(1)}, f32[256,128]{1,0:T(8,128)S(1)}, u32[]{:S(2)}, u32[]{:S(2)}) collective-permute-start(f32[256,128]{1,0:T(8,128)S(1)} %collective-permute-done.5), channel_id=1, source_target_pairs={{0,1},{1,2},{2,3},{3,4},{4,5},{5,6},{6,7},{7,0},{8,9},{9,10},{10,1... | collective-permute-start | bytes 393224 | tf_op jit(solution)/shard_map/ppermute | solution.py:36
  182.5 7.8 %copy-start.2 = (f32[256,128]{1,0:T(8,128)S(1)}, f32[256,128]{1,0:T(8,128)}, u32[]{:S(2)}) copy-start(f32[256,128]{1,0:T(8,128)} %all-reduce.2.cloned.1.call-done) | copy-start | bytes 393220
  189.8 1.0 copy-start.5
Sparse Core Ops, SparseCore 0:
  26.9 74.6 reduce-scatter.1
  103.9 30.6 all-reduce.1
